TPU v7x, 32 devices: a whole 2x2x4 slice. The times are simulated.
32 devices in a mesh: row: 4 (over y, x), col: 8 (over z, core).
Axes of the slice: x: 2, y: 2, z: 4, core: 2. Of those that a mesh axis runs over, the one named last changes fastest.
Arguments:
- basis: bfloat16 [40, 131072], P(None, ('row', 'col'))
- expand: float32 [3, 8, 40], replicated, may hold values from -1 to 1
- tiles: bfloat16 [3, 3072, 128, 128], P(None, ('row', 'col')), may hold values from -0.3125 to 0.3125
- tile_rows: int32 [3072], P(('row', 'col')), may hold values from 0 to 255, as said below
- tile_cols: int32 [3072], P(('row', 'col')), may hold values from 0 to 127
Outputs:
- new_block: float32 [8, 131072], P(None, ('row', 'col'))
- coefficients: float32 [8, 40], replicated
- factor: float32 [8, 8], replicated
Inputs may be any that keep to these rules, and one draw needn't show every extreme that they name: `tile_rows`: each device's 96 tiles come in 8 runs of 12; the row tiles of run k are 12 distinct values from k * 32 to (k + 1) * 32 - 1.
All inputs are finite; a program needn't handle non-finite values.
Results may differ from a plain program's by a relative error of at most 0.0054.
Values may be sent and summed in bfloat16 or wider, within the bound.
A program may use at most 64 MiB of HBM per device.

v0:
```python
import math
import jax
import jax.numpy as jnp
from jax import lax
from jax.sharding import PartitionSpec as P


def shards(basis, expand, tiles, tile_rows, tile_cols):
    highest = lax.Precision.HIGHEST
    row_count = lax.axis_size("row")
    col_count = lax.axis_size("col")
    krylov, length = basis.shape
    tile_size = tiles.shape[2]
    block_size = expand.shape[1]
    entries = length * row_count * col_count
    inverse_root = 1.0 / math.sqrt(entries)
    region = length // tile_size
    basis_full = basis.astype(jnp.float32)
    series = jnp.einsum("mbk,kn->mbn", expand, basis_full, precision=highest).astype(jnp.bfloat16)
    gathered = lax.all_gather(series, "row", axis=2, tiled=True)
    col_tiles = gathered.reshape(3, block_size, row_count * length // tile_size, tile_size)
    picked = jnp.take(col_tiles, tile_cols, axis=2)
    products = jnp.einsum("mtij,mbtj->bti", tiles, picked, preferred_element_type=jnp.float32)
    slot_count = col_count * region
    onehot = (tile_rows[:, None] == jnp.arange(slot_count, dtype=jnp.int32)[None, :]).astype(
        jnp.float32
    )
    partial_value = jnp.einsum("ts,bti->bsi", onehot, products, precision=highest).reshape(
        block_size, slot_count * tile_size
    )
    applied = lax.psum_scatter(partial_value, "col", scatter_dimension=1, tiled=True)
    raw_proj = jnp.dot(applied, basis_full.T, precision=highest) * inverse_root
    correlation = jnp.dot(basis_full, basis_full.T, precision=highest) / entries
    energy = jnp.dot(applied, applied.T, precision=highest)
    first_pass, correlation, energy = lax.psum((raw_proj, correlation, energy), ("row", "col"))
    second_pass = first_pass - jnp.dot(first_pass, correlation, precision=highest)
    coefficients = first_pass + second_pass
    mixed = jnp.dot(first_pass, coefficients.T, precision=highest)
    curved = jnp.dot(
        jnp.dot(coefficients, correlation, precision=highest), coefficients.T, precision=highest
    )
    gram_block = (energy - mixed - mixed.T + curved) / entries
    cleaned = applied - jnp.dot(coefficients, basis_full, precision=highest) * inverse_root
    factor = jnp.linalg.cholesky(gram_block)
    new_block = lax.linalg.triangular_solve(factor, cleaned, left_side=True, lower=True)
    return (new_block, coefficients, factor)


def solution(mesh):
    return jax.shard_map(
        shards,
        mesh=mesh,
        in_specs=(
            P(None, ("row", "col")),
            P(),
            P(None, ("row", "col"), None, None),
            P(("row", "col")),
            P(("row", "col")),
        ),
        out_specs=(P(None, ("row", "col")), P(), P()),
        check_vma=False,
    )
```

profile of v0, /device:TPU:10, one launch (start us, length us, event | category | flops | bytes accessed | tf_op | source)
XLA Modules:
  0.0 118.9 jit_solution(17451722167365213223)
XLA Ops:
  7.2 0.0 copy-start
  7.2 0.0 copy-start.2
  7.2 0.0 reduce-scatter.2.cloned.1.call-start
  7.2 0.7 compare_select_fusion
  7.9 0.7 compare_and_fusion
  8.6 0.0 copy-done
  8.6 1.0 convolution_convert_fusion
  9.6 11.2 %all_gather.3 = bf16[3,8,16384]{2,1,0:T(8,128)(2,1)S(1)} all-gather(bf16[3,8,4096]{2,1,0:T(8,128)(2,1)S(1)} %convolution_convert_fusion), channel_id=1, replica_groups=mesh['row'=4,'col'=8] {'row'}, dimensions={2}, use_global_device_ids=true | all-gather | bytes 983040 | tf_op jit(solution)/shard_map/all_gather | solution.py:20
  20.8 0.8 gather_fusion
  21.6 5.9 %fusion = f32[96,8,128,1]{2,1,3,0:T(8,128)S(1)} fusion(bf16[3,96,128,128]{3,2,1,0:T(8,128)(2,1)} %param.7, bf16[96,3,8,128]{3,2,1,0:T(8,128)(2,1)S(1)} %gather_fusion, pred[96]{0:T(512)(128)(4,1)S(1)} %compare_and_fusion), kind=kOutput, calls=%fused_computation.1 | convolution fusion | flops 75792384 | bytes 10420320 | tf_op jit(solution)/shard_map/mtij,mbtj->bti/dot_general | solution.py:23
  27.5 0.7 convolution_bitcast_fusion
  28.2 0.3 copy.13
  28.5 1.6 %copy.31 = f32[1,8,256,128]{3,1,2,0:T(8,128)} copy(f32[1,8,256,128]{3,2,1,0:T(8,128)S(1)} %bitcast.54) | data formatting | bytes 2097152
  30.1 0.0 reduce-scatter.2.cloned.1.call-update
  30.2 0.2 convolution_multiply_fusion.1
  30.4 29.0 %reduce-scatter.2.cloned.1.call-done = f32[8,4096]{1,0:T(8,128)} async-done(((f32[8,32768]{1,0:T(8,128)}), f32[8,4096]{1,0:T(8,128)}) %reduce-scatter.2.cloned.1.call-update) | async-done | bytes 131088 | tf_op jit(solution)/shard_map/reduce_scatter | solution.py:31
  59.4 1.3 %convolution_multiply_fusion.2 = f32[8,40]{1,0:T(8,128)S(1)} fusion(f32[8,4096]{1,0:T(8,128)} %reduce-scatter.2.cloned.1.call-done, bf16[40,4096]{1,0:T(8,128)(2,1)S(1)} %copy-done), kind=kOutput, calls=%fused_computation.12 | convolution fusion | flops 15728960 | bytes 460032 | tf_op jit(solution)/shard_map/dot_general | solution.py:32
  60.7 1.3 %fusion.19 = f32[8,8]{0,1:T(8,128)S(1)} fusion(f32[8,4096]{1,0:T(8,128)} %reduce-scatter.2.cloned.1.call-done), kind=kOutput, calls=%fused_computation.39 | convolution fusion | flops 3145728 | bytes 131328 | tf_op jit(solution)/shard_map/dot_general | solution.py:34
  62.0 43.9 %all-reduce = (f32[8,40]{1,0:T(8,128)S(1)}, f32[40,40]{1,0:T(8,128)S(1)}, f32[8,8]{0,1:T(8,128)S(1)}) all-reduce(f32[8,40]{1,0:T(8,128)S(1)} %convolution_multiply_fusion.2, f32[40,40]{1,0:T(8,128)S(1)} %convolution_multiply_fusion.1, f32[8,8]{0,1:T(8,128)S(1)} %fusion.19), channel_id=1, replica_groups=mesh['row'=4,'col'=8] {'row','col'}, use_global_device_ids=true, to_apply=%region_2.3 | all-reduce | flops 1984 | bytes 15872 | tf_op jit(solution)/shard_map/psum | solution.py:35
  105.9 0.1 fusion.3
  106.0 0.1 fusion.20
  106.2 0.1 fusion.21
  106.3 0.1 copy.15
  106.4 0.1 fusion.4
  106.5 0.1 copy.17
  106.6 0.7 cholesky.16
  107.3 0.1 select_reduce_fusion
  107.4 0.6 compare_reduce_fusion
  108.0 1.2 %select_bitcast_fusion = (f32[1,8,8]{2,1,0:T(8,128)S(1)}, f32[8,8]{1,0:T(8,128)}) fusion(f32[8,8]{1,0:T(8,128)S(1)} %cholesky.16, pred[]{:T(512)} %compare_reduce_fusion), kind=kLoop, calls=%fused_computation.30 | loop fusion | flops 256 | bytes 769 | tf_op jit(solution)/shard_map/triangular_solve | solution.py:45
  109.3 0.6 custom-call.6
  109.9 1.2 fusion.2
  111.1 1.0 fusion.15
  (5 shorter events, 0.0 us)
Async XLA Ops:
  7.2 1.4 %copy-start = (bf16[40,4096]{1,0:T(8,128)(2,1)S(1)}, bf16[40,4096]{1,0:T(8,128)(2,1)}, u32[]{:S(2)}) copy-start(bf16[40,4096]{1,0:T(8,128)(2,1)} %param.5) | copy-start | bytes 983044
  7.2 20.3 %copy-start.2 = (s32[96]{0:T(128)S(1)}, s32[96]{0:T(128)}, u32[]{:S(2)}) copy-start(s32[96]{0:T(128)} %param.8) | copy-start | bytes 1156
  7.2 52.2 %reduce-scatter.2.cloned.1.call-start = ((), (), s32[]{:S(2)}) async-start(), calls=%async_computation.1 | async-start | bytes 1179648 | tf_op jit(solution)/shard_map/reduce_scatter | solution.py:31
  106.0 6.0 %copy-start.1 = (f32[8,40]{1,0:T(8,128)}, f32[8,40]{1,0:T(8,128)S(1)}, u32[]{:S(2)}) copy-start(f32[8,40]{1,0:T(8,128)S(1)} %fusion.3) | copy-start | bytes 3844
Sparse Core Ops, SparseCore 0:
  30.3 29.0 reduce-scatter.1
where the time goes:
time: 119 us
  blocking collectives  55.1 us (46%)
  waiting for transfers between devices  29 us (24%)
  between operations  14.1 us (12%)
  matrix products  13.1 us (11%)
  other arithmetic  4.65 us (4%)
  local copies, waits for them, and re-layouts  2.88 us (2%)
    psum x1, blocking collectives, shards(): lax.psum((raw_proj, correlation, energy), ('row', 'col'))  43.9 us
    reduce_scatter x1, waiting for transfers between devices, shards(): lax.psum_scatter(partial_value, 'col', scatter_dimension=1, tiled=True)  29 us
    all_gather x1, blocking collectives, shards(): gathered = lax.all_gather(series, 'row', axis=2, tiled=True)  11.2 us
    dot_general x1, matrix products, shards(): jnp.einsum('mtij,mbtj->bti', tiles, picked, preferred_element_type=jnp.fl...  5.9 us
  transfers between devices with their start and end apart: 1, of which 1 were waited for; matrix products, arithmetic and copies ran while one was open for 0% of the time, Pallas kernels for 0%

commit v1 on v0

--- a/solution.py
+++ b/solution.py
@@ -17,7 +17,17 @@
     region = length // tile_size
     basis_full = basis.astype(jnp.float32)
     series = jnp.einsum("mbk,kn->mbn", expand, basis_full, precision=highest).astype(jnp.bfloat16)
-    gathered = lax.all_gather(series, "row", axis=2, tiled=True)
+    devs = lax.axis_size("row")
+    arr_now = sorted(((j, (j + 1) % devs) for j in range(devs)))
+    r1 = series
+    grid = [r1]
+    for no in tuple(range(1, devs)):
+        r1 = lax.ppermute(r1, "row", arr_now)
+        grid.insert(0, r1)
+    spare = jnp.concatenate(grid, axis=2)
+    current_value = lax.axis_index("row")
+    t1 = current_value + 1
+    gathered = jnp.roll(spare, t1 * series.shape[2], axis=2)
     col_tiles = gathered.reshape(3, block_size, row_count * length // tile_size, tile_size)
     picked = jnp.take(col_tiles, tile_cols, axis=2)
     products = jnp.einsum("mtij,mbtj->bti", tiles, picked, preferred_element_type=jnp.float32)

time: 119 us -> 129 us (1.084)
  waiting for transfers between devices: 29 us -> 41.4 us
  blocking collectives: 55.1 us -> 43.8 us
  starting transfers between devices: 0.04 us -> 7.24 us
    all_gather x1 -> x0, blocking collectives: 11.2 us -> none  [shards(): gathered = lax.all_gather(series, 'row', axis=2, tiled=True)]
    ppermute x0 -> x3, waiting for transfers between devices: none -> 10.4 us  [shards(): r1 = lax.ppermute(r1, 'row', arr_now)]
    ppermute x0 -> x3, starting transfers between devices: none -> 7.21 us  [shards(): r1 = lax.ppermute(r1, 'row', arr_now)]
    reduce_scatter x1, waiting for transfers between devices: 29 us -> 31 us  [shards(): lax.psum_scatter(partial_value, 'col', scatter_dimension=1, tiled=True)]
    unnamed x7 -> x14, local copies, waits for them, and re-layouts: 1.62 us -> 2.65 us
  transfers between devices with their start and end apart: 1 -> 4, of which waited for: 1 -> 4; matrix products, arithmetic and copies ran while one was open for 0% -> 1% of each run, Pallas kernels for 0% -> 0%
where the time goes in v1:
time: 129 us; the launch traced here: 128 us
  blocking collectives  43.8 us (34%)
  waiting for transfers between devices  41.4 us (32%)
  between operations  14.2 us (11%)
  matrix products  13.1 us (10%)
  starting transfers between devices  7.24 us (6%)
  other arithmetic  4.61 us (4%)
  local copies, waits for them, and re-layouts  3.98 us (3%)
    psum x1, blocking collectives, shards(): lax.psum((raw_proj, correlation, energy), ('row', 'col'))  43.8 us
    reduce_scatter x1, waiting for transfers between devices, shards(): lax.psum_scatter(partial_value, 'col', scatter_dimension=1, tiled=True)  31 us
    ppermute x3, waiting for transfers between devices, shards(): r1 = lax.ppermute(r1, 'row', arr_now)  10.4 us
    ppermute x3, starting transfers between devices, shards(): r1 = lax.ppermute(r1, 'row', arr_now)  7.21 us
    dot_general x1, matrix products, shards(): jnp.einsum('mtij,mbtj->bti', tiles, picked, preferred_element_type=jnp.fl...  5.9 us
    unnamed x14, local copies, waits for them, and re-layouts  2.65 us
  transfers between devices with their start and end apart: 4, of which 4 were waited for; matrix products, arithmetic and copies ran while one was open for 1% of the time, Pallas kernels for 0%

profile of v1, /device:TPU:10, one launch (start us, length us, event | category | flops | bytes accessed | tf_op | source)
XLA Modules:
  0.0 128.4 jit_solution(3646461074901886381)
XLA Ops:
  7.2 0.9 copy-done
  8.1 1.0 convolution_convert_fusion
  9.2 1.5 %collective-permute-start = (bf16[3,8,4096]{2,1,0:T(8,128)(2,1)S(1)}, bf16[3,8,4096]{2,1,0:T(8,128)(2,1)S(1)}, u32[]{:S(2)}, u32[]{:S(2)}) collective-permute-start(bf16[3,8,4096]{2,1,0:T(8,128)(2,1)S(1)} %convolution_convert_fusion), channel_id=1, source_target_pairs={{0,8},{8,16},{16,24},{24,0},{1,9},{9,17},{17,25},{25,1},{2,10},{10... | collective-permute-start | bytes 589832 | tf_op jit(solution)/shard_map/ppermute | solution.py:25
  10.7 5.2 %collective-permute-done = bf16[3,8,4096]{2,1,0:T(8,128)(2,1)S(1)} collective-permute-done((bf16[3,8,4096]{2,1,0:T(8,128)(2,1)S(1)}, bf16[3,8,4096]{2,1,0:T(8,128)(2,1)S(1)}, u32[]{:S(2)}, u32[]{:S(2)}) %collective-permute-start) | collective-permute-done | bytes 196640 | tf_op jit(solution)/shard_map/ppermute | solution.py:25
  15.9 2.4 %collective-permute-start.1 = (bf16[3,8,4096]{2,1,0:T(8,128)(2,1)S(1)}, bf16[3,8,4096]{2,1,0:T(8,128)(2,1)S(1)}, u32[]{:S(2)}, u32[]{:S(2)}) collective-permute-start(bf16[3,8,4096]{2,1,0:T(8,128)(2,1)S(1)} %collective-permute-done), channel_id=1, source_target_pairs={{0,8},{8,16},{16,24},{24,0},{1,9},{9,17},{17,25},{25,1},{2,10},{10... | collective-permute-start | bytes 589832 | tf_op jit(solution)/shard_map/ppermute | solution.py:25
  18.2 0.7 compare_select_fusion
  18.9 2.7 %collective-permute-done.1 = bf16[3,8,4096]{2,1,0:T(8,128)(2,1)S(1)} collective-permute-done((bf16[3,8,4096]{2,1,0:T(8,128)(2,1)S(1)}, bf16[3,8,4096]{2,1,0:T(8,128)(2,1)S(1)}, u32[]{:S(2)}, u32[]{:S(2)}) %collective-permute-start.1) | collective-permute-done | bytes 196640 | tf_op jit(solution)/shard_map/ppermute | solution.py:25
  21.6 3.3 %collective-permute-start.2 = (bf16[3,8,4096]{2,1,0:T(8,128)(2,1)S(1)}, bf16[3,8,4096]{2,1,0:T(8,128)(2,1)S(1)}, u32[]{:S(2)}, u32[]{:S(2)}) collective-permute-start(bf16[3,8,4096]{2,1,0:T(8,128)(2,1)S(1)} %collective-permute-done.1), channel_id=1, source_target_pairs={{0,8},{8,16},{16,24},{24,0},{1,9},{9,17},{17,25},{25,1},{2,10},{10... | collective-permute-start | bytes 589832 | tf_op jit(solution)/shard_map/ppermute | solution.py:25
  24.9 0.7 compare_and_fusion
  25.6 2.5 %collective-permute-done.2 = bf16[3,8,4096]{2,1,0:T(8,128)(2,1)S(1)} collective-permute-done((bf16[3,8,4096]{2,1,0:T(8,128)(2,1)S(1)}, bf16[3,8,4096]{2,1,0:T(8,128)(2,1)S(1)}, u32[]{:S(2)}, u32[]{:S(2)}) %collective-permute-start.2) | collective-permute-done | bytes 196640 | tf_op jit(solution)/shard_map/ppermute | solution.py:25
  28.4 0.8 gather_fusion
  29.2 5.9 %fusion = f32[96,8,128,1]{2,1,3,0:T(8,128)S(1)} fusion(bf16[3,96,128,128]{3,2,1,0:T(8,128)(2,1)} %param.7, bf16[96,3,8,128]{3,2,1,0:T(8,128)(2,1)S(1)} %gather_fusion, pred[96]{0:T(512)(128)(4,1)S(1)} %compare_and_fusion), kind=kOutput, calls=%fused_computation.1 | convolution fusion | flops 75792384 | bytes 10420320 | tf_op jit(solution)/shard_map/mtij,mbtj->bti/dot_general | solution.py:33
  35.1 0.7 convolution_bitcast_fusion
  35.7 0.3 copy.13
  36.1 1.6 %copy.31 = f32[1,8,256,128]{3,1,2,0:T(8,128)} copy(f32[1,8,256,128]{3,2,1,0:T(8,128)S(1)} %bitcast.55) | data formatting | bytes 2097152
  37.7 0.2 convolution_multiply_fusion.1
  37.9 31.0 %reduce-scatter.2.cloned.1.call-done = f32[8,4096]{1,0:T(8,128)} async-done(((f32[8,32768]{1,0:T(8,128)}), f32[8,4096]{1,0:T(8,128)}) %reduce-scatter.2.cloned.1.call-update) | async-done | bytes 131088 | tf_op jit(solution)/shard_map/reduce_scatter | solution.py:41
  68.9 1.3 convolution_multiply_fusion.2
  70.2 1.3 %fusion.19 = f32[8,8]{0,1:T(8,128)S(1)} fusion(f32[8,4096]{1,0:T(8,128)} %reduce-scatter.2.cloned.1.call-done), kind=kOutput, calls=%fused_computation.48 | convolution fusion | flops 3145728 | bytes 131328 | tf_op jit(solution)/shard_map/dot_general | solution.py:44
  71.5 43.8 %all-reduce = (f32[8,40]{1,0:T(8,128)S(1)}, f32[40,40]{1,0:T(8,128)S(1)}, f32[8,8]{0,1:T(8,128)S(1)}) all-reduce(f32[8,40]{1,0:T(8,128)S(1)} %convolution_multiply_fusion.2, f32[40,40]{1,0:T(8,128)S(1)} %convolution_multiply_fusion.1, f32[8,8]{0,1:T(8,128)S(1)} %fusion.19), channel_id=1, replica_groups=mesh['row'=4,'col'=8] {'row','col'}, use_global_device_ids=true, to_apply=%region_2.3 | all-reduce | flops 1984 | bytes 15872 | tf_op jit(solution)/shard_map/psum | solution.py:45
  115.4 0.1 fusion.3
  115.5 0.1 fusion.21
  115.6 0.1 fusion.20
  115.8 0.1 copy.15
  115.8 0.1 fusion.4
  116.0 0.1 copy.17
  116.1 0.7 cholesky.16
  116.8 0.6 compare_reduce_fusion
  117.5 1.2 select_bitcast_fusion
  118.7 0.6 custom-call.6
  119.3 1.2 fusion.2
  120.5 1.0 fusion.15
  (19 shorter events, 0.3 us)
Async XLA Ops:
  7.2 1.0 copy-start
  7.2 61.7 %reduce-scatter.2.cloned.1.call-start = ((), (), s32[]{:S(2)}) async-start(), calls=%async_computation.1 | async-start | bytes 1179648 | tf_op jit(solution)/shard_map/reduce_scatter | solution.py:41
  9.2 6.7 %collective-permute-start = (bf16[3,8,4096]{2,1,0:T(8,128)(2,1)S(1)}, bf16[3,8,4096]{2,1,0:T(8,128)(2,1)S(1)}, u32[]{:S(2)}, u32[]{:S(2)}) collective-permute-start(bf16[3,8,4096]{2,1,0:T(8,128)(2,1)S(1)} %convolution_convert_fusion), channel_id=1, source_target_pairs={{0,8},{8,16},{16,24},{24,0},{1,9},{9,17},{17,25},{25,1},{2,10},{10... | collective-permute-start | bytes 589832 | tf_op jit(solution)/shard_map/ppermute | solution.py:25
  15.9 5.8 %collective-permute-start.1 = (bf16[3,8,4096]{2,1,0:T(8,128)(2,1)S(1)}, bf16[3,8,4096]{2,1,0:T(8,128)(2,1)S(1)}, u32[]{:S(2)}, u32[]{:S(2)}) collective-permute-start(bf16[3,8,4096]{2,1,0:T(8,128)(2,1)S(1)} %collective-permute-done), channel_id=1, source_target_pairs={{0,8},{8,16},{16,24},{24,0},{1,9},{9,17},{17,25},{25,1},{2,10},{10... | collective-permute-start | bytes 589832 | tf_op jit(solution)/shard_map/ppermute | solution.py:25
  21.6 6.5 %collective-permute-start.2 = (bf16[3,8,4096]{2,1,0:T(8,128)(2,1)S(1)}, bf16[3,8,4096]{2,1,0:T(8,128)(2,1)S(1)}, u32[]{:S(2)}, u32[]{:S(2)}) collective-permute-start(bf16[3,8,4096]{2,1,0:T(8,128)(2,1)S(1)} %collective-permute-done.1), channel_id=1, source_target_pairs={{0,8},{8,16},{16,24},{24,0},{1,9},{9,17},{17,25},{25,1},{2,10},{10... | collective-permute-start | bytes 589832 | tf_op jit(solution)/shard_map/ppermute | solution.py:25
  29.2 5.9 %copy-start.2 = (s32[96]{0:T(128)S(1)}, s32[96]{0:T(128)}, u32[]{:S(2)}) copy-start(s32[96]{0:T(128)} %param.8) | copy-start | bytes 1156
  115.5 6.0 %copy-start.1 = (f32[8,40]{1,0:T(8,128)}, f32[8,40]{1,0:T(8,128)S(1)}, u32[]{:S(2)}) copy-start(f32[8,40]{1,0:T(8,128)S(1)} %fusion.3) | copy-start | bytes 3844
Sparse Core Ops, SparseCore 0:
  37.8 31.0 reduce-scatter.1
